TPU v7x, 512 devices: a 8x2x16 block of a 8x16x16 slice. The times are simulated.
512 devices in a mesh: groups: 2 (over y), tok: 16 (over z), head: 8 (over x), row: 2 (over core).
Axes of the slice: x: 8, y: 2, z: 16, core: 2. Of those that a mesh axis runs over, the one named last changes fastest.
The devices are a block of a 8x16x16 slice.
Arguments:
- text: bfloat16 [1024, 8192], P(('groups', 'row'), 'tok'), parts along dimension 0, may hold values from -12 to 12
- q_weight: bfloat16 [8192, 8192], P('tok', 'head'), may hold values from -0.0625 to 0.0625
- out_weight: bfloat16 [8192, 8192], P('head', 'tok'), may hold values from -0.0625 to 0.0625
- keys: bfloat16 [131072, 1024], P(('groups', 'tok'), 'head'), parts along dimension 0, may hold values from -60 to 60
- values: bfloat16 [131072, 1024], P(('groups', 'tok'), 'head'), parts along dimension 0, may hold values from -6 to 6
- gate: float32 [1], replicated, may hold values from 0.3 to 1.5
Outputs:
- result: bfloat16 [1024, 8192], P(('groups', 'row'), 'tok'), parts along dimension 0
There are 2 independent parts, one for each index of `groups`. A program takes and returns all parts, laid end to end along the dimension named above; an argument that names none is the same for every part. Nothing has to cross between parts.
All inputs are finite; a program needn't handle non-finite values.
Results may differ from a plain program's by a relative error of at most 0.015.
Values may be sent and summed in bfloat16 or wider, within the bound.
A program may use at most 64 MiB of HBM per device.

v0:
```python
import jax
import jax.numpy as jnp
from jax import lax
from jax.sharding import PartitionSpec as P

HD = 128
GROUP = 8


def copy_for_each(array, axis):
    devices = lax.axis_size(axis)
    return lax.all_to_all(
        jnp.broadcast_to(array[None], (devices, *array.shape)), axis, 0, 0, tiled=True
    )


def taken_together(array, axis):
    return copy_for_each(array, axis).sum(axis=0)


def cut_along(array, dim, devices):
    lengths = array.shape
    parts = array.reshape(*lengths[:dim], devices, lengths[dim] // devices, *lengths[dim + 1 :])
    return jnp.moveaxis(parts, dim, 0)


def sum_at_owner(array, axis, dim):
    parts = cut_along(array, dim, lax.axis_size(axis))
    arrived = lax.all_to_all(parts, axis, split_axis=0, concat_axis=0, tiled=True)
    return arrived.astype(jnp.float32).sum(axis=0)


def side_by_side(arrays, axis, split_dim, concat_dim, along):
    columns = [a.reshape(*a.shape[:along], -1) for a in arrays]
    both = jnp.concatenate(columns, axis=along)
    out, at, outs = (
        lax.all_to_all(both, axis, split_axis=split_dim, concat_axis=concat_dim, tiled=True),
        0,
        [],
    )
    for a, column in zip(arrays, columns):
        piece = out[..., at : at + column.shape[along]]
        outs.append(piece.reshape(*piece.shape[:along], *a.shape[along:]))
        at += column.shape[along]
    return tuple(outs)


def joined_along(parts, dim):
    parts = jnp.moveaxis(parts, 0, dim)
    lengths = parts.shape
    return parts.reshape(*lengths[:dim], lengths[dim] * lengths[dim + 1], *lengths[dim + 2 :])


def gathered_copies(array, axis, dim):
    return joined_along(copy_for_each(array, axis), dim)


def attend(queries, keys, values, carry):
    tokens = keys.shape[0]
    local_kv = keys.shape[1] // HD
    size = min(512, tokens)
    key_blocks = keys.reshape(tokens // size, size, local_kv, HD)
    value_blocks = values.reshape(tokens // size, size, local_kv, HD)

    def step(state, pair):
        running, total, accum = state
        key_block, value_block = pair
        scores = jnp.einsum(
            "rkgd,skd->krgs", queries, key_block, preferred_element_type=jnp.float32
        )
        newmax = jnp.maximum(running, jnp.max(scores, axis=3))
        weights = jnp.exp(scores - newmax[..., None])
        factor = jnp.exp(running - newmax)
        total = total * factor + jnp.sum(weights, axis=3)
        rounded = weights.astype(jnp.bfloat16)
        accum = accum * factor[..., None] + jnp.einsum(
            "krgs,skd->krgd", rounded, value_block, preferred_element_type=jnp.float32
        )
        return ((newmax, total, accum), None)

    carry, _ = lax.scan(step, carry, (key_blocks, value_blocks))
    return carry


def empty_state(rows, local_kv):
    return (
        jnp.full((local_kv, rows, GROUP), -1e30, jnp.float32),
        jnp.zeros((local_kv, rows, GROUP), jnp.float32),
        jnp.zeros((local_kv, rows, GROUP, HD), jnp.float32),
    )


def finalize(state):
    running, total, accum = state
    outputs = accum / total[..., None]
    local_kv, rows = (outputs.shape[0], outputs.shape[1])
    return (
        jnp.transpose(outputs, (1, 0, 2, 3))
        .reshape(rows, local_kv * GROUP * HD)
        .astype(jnp.bfloat16)
    )


def body(text, q_weight, out_weight, keys, values, gate):
    hidden = text.astype(jnp.float32)
    squares = taken_together(jnp.sum(hidden * hidden, axis=1), "tok")
    features = hidden.shape[1] * lax.axis_size("tok")
    normed = (hidden * lax.rsqrt(squares / features + 1e-05)[:, None]).astype(jnp.bfloat16)
    local_kv = keys.shape[1] // HD
    share_rows = normed.shape[0] // lax.axis_size("tok")
    picked = normed
    projected = sum_at_owner(
        jnp.dot(picked, q_weight, preferred_element_type=jnp.float32).astype(jnp.bfloat16), "tok", 0
    )
    rows = projected.shape[0]
    view = projected.reshape(rows, local_kv, GROUP, HD)
    share_queries = (view / jnp.sqrt(jnp.float32(HD))).astype(jnp.bfloat16)
    queries = lax.all_gather(share_queries, "tok", axis=0, tiled=True)
    running, total, accum = attend(queries, keys, values, empty_state(normed.shape[0], local_kv))
    pieces = tuple(
        (
            part.astype(jnp.float32)
            for part in side_by_side(
                (
                    running[None].astype(jnp.bfloat16),
                    total[None].astype(jnp.bfloat16),
                    accum[None].astype(jnp.bfloat16),
                ),
                "tok",
                2,
                0,
                4,
            )
        )
    )
    piece_max, piece_total, piece_accum = pieces
    newmax = jnp.max(piece_max, axis=0)
    factor = jnp.exp(piece_max - newmax[None])
    merged_total = jnp.sum(piece_total * factor, axis=0)
    merged_accum = jnp.sum(piece_accum * factor[..., None], axis=0)
    share_attended = finalize((newmax, merged_total, merged_accum))
    attended = gathered_copies(share_attended, "tok", 0)
    strength = jnp.tanh(gate[0])
    share_rows = attended.shape[0] // lax.axis_size("head")
    picked = attended
    branch = sum_at_owner(
        jnp.dot(picked, out_weight, preferred_element_type=jnp.float32).astype(jnp.bfloat16),
        "head",
        0,
    )
    offset = lax.axis_index("head") * share_rows
    mine = lax.dynamic_slice_in_dim(hidden, offset, share_rows, 0)
    finished = (mine + strength * branch).astype(jnp.bfloat16)
    return gathered_copies(finished, "head", 0)


def solution(mesh):
    in_specs = (
        P(("groups", "row"), "tok"),
        P("tok", "head"),
        P("head", "tok"),
        P(("groups", "tok"), "head"),
        P(("groups", "tok"), "head"),
        P(),
    )
    out_specs = P(("groups", "row"), "tok")
    return jax.shard_map(body, mesh=mesh, in_specs=in_specs, out_specs=out_specs, check_vma=False)
```

profile of v0, /device:TPU:80, one launch (start us, length us, event | category | flops | bytes accessed | tf_op | source)
XLA Modules:
  0.0 306.5 jit_solution(6369199125377583567)
XLA Ops:
  0.0 1.2 multiply_reduce_fusion.1
  1.2 55.8 %all_to_all.38 = f32[16,1,256]{2,1,0:T(1,128)S(1)} all-to-all(f32[16,1,256]{2,1,0:T(1,128)S(1)} %broadcast_in_dim.17), channel_id=1, replica_groups=mesh['groups'=2,'tok'=16,'head'=8,'row'=2] {'tok'}, dimensions={0} | all-to-all | bytes 32768 | tf_op jit(solution)/shard_map/all_to_all | solution.py:12
  57.0 2.2 convolution_convert_fusion
  59.3 4.0 %all-to-all-start.1 = ((bf16[16,16,1024]{2,1,0:T(8,128)(2,1)}), bf16[16,16,1024]{2,1,0:T(8,128)(2,1)S(1)}, u32[]{:S(2)}, u32[]{:S(2)}) async-start(bf16[16,16,1024]{2,1,0:T(8,128)(2,1)} %bitcast.2), calls=%async_computation.1 | async-start | bytes 1048576 | tf_op jit(solution)/shard_map/all_to_all | solution.py:29
  63.3 26.8 %all-to-all-done.1 = bf16[16,16,1024]{2,1,0:T(8,128)(2,1)S(1)} async-done(((bf16[16,16,1024]{2,1,0:T(8,128)(2,1)}), bf16[16,16,1024]{2,1,0:T(8,128)(2,1)S(1)}, u32[]{:S(2)}, u32[]{:S(2)}) %all-to-all-start.1) | async-done | bytes 524320 | tf_op jit(solution)/shard_map/all_to_all | solution.py:29
  90.2 34.1 %all_gather.3 = bf16[256,1,8,128]{3,2,1,0:T(8,128)(2,1)S(1)} all-gather(bf16[16,1,8,128]{3,2,1,0:T(8,128)(2,1)S(1)} %bitcast.116), channel_id=1, replica_groups=mesh['groups'=2,'tok'=16,'head'=8,'row'=2] {'tok'}, dimensions={0}, use_global_device_ids=true | all-gather | bytes 557056 | tf_op jit(solution)/shard_map/all_gather | solution.py:118
  124.4 64.2 %while.15 = (s32[]{:T(128)}, f32[1,256,8]{1,2,0:T(8,128)S(1)}, f32[1,256,8]{1,2,0:T(8,128)S(1)}, f32[1,256,8,128]{3,1,2,0:T(8,128)S(1)}, bf16[8,512,1,128]{3,1,2...) while((s32[]{:T(128)}, f32[1,256,8]{1,2,0:T(8,128)S(1)}, ...), condition=%wide.region_6.7_spmd.clone, body=%wide.region_3.6_spmd.clone.sunk | while | flops 542912512 | bytes 32375940 | solution.py:81
  124.4 3.5 %bitcast_reduce_fusion.2 = (f32[256,8]{0,1:T(8,128)S(1)}, f32[512,256,8]{1,0,2:T(8,128)}) fusion(bf16[256,1,8,128]{3,0,2,1:T(8,128)(2,1)S(1)} %get-tuple-element.217, bf16[8,512,1,128]{3,1,2,0:T(8,128)(2,1)} %get-tuple-element.216, s32[]{:T(128)} %get-tuple-element.203), kind=kOutput, calls=%fused_computation.1.clone.1 | convolution fusion | flops 269481984 | bytes 4858368 | tf_op jit(solution)/shard_map/while/body/eval_jaxpr/rkgd,skd->krgs/dot_general | solution.py:68
  128.0 3.8 %fusion.44 = f32[1,256,8,128]{3,1,2,0:T(8,128)S(1)} fusion(f32[512,256,8]{1,0,2:T(8,128)} %get-tuple-element.192, f32[256,8]{0,1:T(8,128)S(1)} %bitcast.109, f32[1,256,8,128]{3,1,2,0:T(8,128)S(1)} %get-tuple-element.206, f32[256,8]{0,1:T(8,128)S(1)} %get-tuple-element.193, pred[]{:T(512)S(6)} %compare.3, ...), kind=kOutput, calls=%fused_computation.8.clone.1 | convolution fusion | flops 271319040 | bytes 6439425 | tf_op jit(solution)/shard_map/while/body/eval_jaxpr/krgs,skd->krgd/dot_general | solution.py:76
  131.8 0.6 fusion.43
  132.4 3.5 %bitcast_reduce_fusion.2 = (f32[256,8]{0,1:T(8,128)S(1)}, f32[512,256,8]{1,0,2:T(8,128)}) fusion(bf16[256,1,8,128]{3,0,2,1:T(8,128)(2,1)S(1)} %get-tuple-element.217, bf16[8,512,1,128]{3,1,2,0:T(8,128)(2,1)} %get-tuple-element.216, s32[]{:T(128)} %get-tuple-element.203), kind=kOutput, calls=%fused_computation.1.clone.1 | convolution fusion | flops 269481984 | bytes 4858368 | tf_op jit(solution)/shard_map/while/body/eval_jaxpr/rkgd,skd->krgs/dot_general | solution.py:68
  136.0 3.8 %fusion.44 = f32[1,256,8,128]{3,1,2,0:T(8,128)S(1)} fusion(f32[512,256,8]{1,0,2:T(8,128)} %get-tuple-element.192, f32[256,8]{0,1:T(8,128)S(1)} %bitcast.109, f32[1,256,8,128]{3,1,2,0:T(8,128)S(1)} %get-tuple-element.206, f32[256,8]{0,1:T(8,128)S(1)} %get-tuple-element.193, pred[]{:T(512)S(6)} %compare.3, ...), kind=kOutput, calls=%fused_computation.8.clone.1 | convolution fusion | flops 271319040 | bytes 6439425 | tf_op jit(solution)/shard_map/while/body/eval_jaxpr/krgs,skd->krgd/dot_general | solution.py:76
  139.8 0.6 fusion.43
  140.4 3.5 %bitcast_reduce_fusion.2 = (f32[256,8]{0,1:T(8,128)S(1)}, f32[512,256,8]{1,0,2:T(8,128)}) fusion(bf16[256,1,8,128]{3,0,2,1:T(8,128)(2,1)S(1)} %get-tuple-element.217, bf16[8,512,1,128]{3,1,2,0:T(8,128)(2,1)} %get-tuple-element.216, s32[]{:T(128)} %get-tuple-element.203), kind=kOutput, calls=%fused_computation.1.clone.1 | convolution fusion | flops 269481984 | bytes 4858368 | tf_op jit(solution)/shard_map/while/body/eval_jaxpr/rkgd,skd->krgs/dot_general | solution.py:68
  144.0 3.8 %fusion.44 = f32[1,256,8,128]{3,1,2,0:T(8,128)S(1)} fusion(f32[512,256,8]{1,0,2:T(8,128)} %get-tuple-element.192, f32[256,8]{0,1:T(8,128)S(1)} %bitcast.109, f32[1,256,8,128]{3,1,2,0:T(8,128)S(1)} %get-tuple-element.206, f32[256,8]{0,1:T(8,128)S(1)} %get-tuple-element.193, pred[]{:T(512)S(6)} %compare.3, ...), kind=kOutput, calls=%fused_computation.8.clone.1 | convolution fusion | flops 271319040 | bytes 6439425 | tf_op jit(solution)/shard_map/while/body/eval_jaxpr/krgs,skd->krgd/dot_general | solution.py:76
  147.8 0.6 fusion.43
  148.5 3.5 %bitcast_reduce_fusion.2 = (f32[256,8]{0,1:T(8,128)S(1)}, f32[512,256,8]{1,0,2:T(8,128)}) fusion(bf16[256,1,8,128]{3,0,2,1:T(8,128)(2,1)S(1)} %get-tuple-element.217, bf16[8,512,1,128]{3,1,2,0:T(8,128)(2,1)} %get-tuple-element.216, s32[]{:T(128)} %get-tuple-element.203), kind=kOutput, calls=%fused_computation.1.clone.1 | convolution fusion | flops 269481984 | bytes 4858368 | tf_op jit(solution)/shard_map/while/body/eval_jaxpr/rkgd,skd->krgs/dot_general | solution.py:68
  152.0 3.8 %fusion.44 = f32[1,256,8,128]{3,1,2,0:T(8,128)S(1)} fusion(f32[512,256,8]{1,0,2:T(8,128)} %get-tuple-element.192, f32[256,8]{0,1:T(8,128)S(1)} %bitcast.109, f32[1,256,8,128]{3,1,2,0:T(8,128)S(1)} %get-tuple-element.206, f32[256,8]{0,1:T(8,128)S(1)} %get-tuple-element.193, pred[]{:T(512)S(6)} %compare.3, ...), kind=kOutput, calls=%fused_computation.8.clone.1 | convolution fusion | flops 271319040 | bytes 6439425 | tf_op jit(solution)/shard_map/while/body/eval_jaxpr/krgs,skd->krgd/dot_general | solution.py:76
  155.9 0.6 fusion.43
  156.5 3.5 %bitcast_reduce_fusion.2 = (f32[256,8]{0,1:T(8,128)S(1)}, f32[512,256,8]{1,0,2:T(8,128)}) fusion(bf16[256,1,8,128]{3,0,2,1:T(8,128)(2,1)S(1)} %get-tuple-element.217, bf16[8,512,1,128]{3,1,2,0:T(8,128)(2,1)} %get-tuple-element.216, s32[]{:T(128)} %get-tuple-element.203), kind=kOutput, calls=%fused_computation.1.clone.1 | convolution fusion | flops 269481984 | bytes 4858368 | tf_op jit(solution)/shard_map/while/body/eval_jaxpr/rkgd,skd->krgs/dot_general | solution.py:68
  160.0 3.8 %fusion.44 = f32[1,256,8,128]{3,1,2,0:T(8,128)S(1)} fusion(f32[512,256,8]{1,0,2:T(8,128)} %get-tuple-element.192, f32[256,8]{0,1:T(8,128)S(1)} %bitcast.109, f32[1,256,8,128]{3,1,2,0:T(8,128)S(1)} %get-tuple-element.206, f32[256,8]{0,1:T(8,128)S(1)} %get-tuple-element.193, pred[]{:T(512)S(6)} %compare.3, ...), kind=kOutput, calls=%fused_computation.8.clone.1 | convolution fusion | flops 271319040 | bytes 6439425 | tf_op jit(solution)/shard_map/while/body/eval_jaxpr/krgs,skd->krgd/dot_general | solution.py:76
  163.9 0.6 fusion.43
  164.5 3.5 %bitcast_reduce_fusion.2 = (f32[256,8]{0,1:T(8,128)S(1)}, f32[512,256,8]{1,0,2:T(8,128)}) fusion(bf16[256,1,8,128]{3,0,2,1:T(8,128)(2,1)S(1)} %get-tuple-element.217, bf16[8,512,1,128]{3,1,2,0:T(8,128)(2,1)} %get-tuple-element.216, s32[]{:T(128)} %get-tuple-element.203), kind=kOutput, calls=%fused_computation.1.clone.1 | convolution fusion | flops 269481984 | bytes 4858368 | tf_op jit(solution)/shard_map/while/body/eval_jaxpr/rkgd,skd->krgs/dot_general | solution.py:68
  168.1 3.8 %fusion.44 = f32[1,256,8,128]{3,1,2,0:T(8,128)S(1)} fusion(f32[512,256,8]{1,0,2:T(8,128)} %get-tuple-element.192, f32[256,8]{0,1:T(8,128)S(1)} %bitcast.109, f32[1,256,8,128]{3,1,2,0:T(8,128)S(1)} %get-tuple-element.206, f32[256,8]{0,1:T(8,128)S(1)} %get-tuple-element.193, pred[]{:T(512)S(6)} %compare.3, ...), kind=kOutput, calls=%fused_computation.8.clone.1 | convolution fusion | flops 271319040 | bytes 6439425 | tf_op jit(solution)/shard_map/while/body/eval_jaxpr/krgs,skd->krgd/dot_general | solution.py:76
  171.9 0.6 fusion.43
  172.5 3.5 %bitcast_reduce_fusion.2 = (f32[256,8]{0,1:T(8,128)S(1)}, f32[512,256,8]{1,0,2:T(8,128)}) fusion(bf16[256,1,8,128]{3,0,2,1:T(8,128)(2,1)S(1)} %get-tuple-element.217, bf16[8,512,1,128]{3,1,2,0:T(8,128)(2,1)} %get-tuple-element.216, s32[]{:T(128)} %get-tuple-element.203), kind=kOutput, calls=%fused_computation.1.clone.1 | convolution fusion | flops 269481984 | bytes 4858368 | tf_op jit(solution)/shard_map/while/body/eval_jaxpr/rkgd,skd->krgs/dot_general | solution.py:68
  176.1 3.8 %fusion.44 = f32[1,256,8,128]{3,1,2,0:T(8,128)S(1)} fusion(f32[512,256,8]{1,0,2:T(8,128)} %get-tuple-element.192, f32[256,8]{0,1:T(8,128)S(1)} %bitcast.109, f32[1,256,8,128]{3,1,2,0:T(8,128)S(1)} %get-tuple-element.206, f32[256,8]{0,1:T(8,128)S(1)} %get-tuple-element.193, pred[]{:T(512)S(6)} %compare.3, ...), kind=kOutput, calls=%fused_computation.8.clone.1 | convolution fusion | flops 271319040 | bytes 6439425 | tf_op jit(solution)/shard_map/while/body/eval_jaxpr/krgs,skd->krgd/dot_general | solution.py:76
  179.9 0.6 fusion.43
  180.5 3.5 %bitcast_reduce_fusion.2 = (f32[256,8]{0,1:T(8,128)S(1)}, f32[512,256,8]{1,0,2:T(8,128)}) fusion(bf16[256,1,8,128]{3,0,2,1:T(8,128)(2,1)S(1)} %get-tuple-element.217, bf16[8,512,1,128]{3,1,2,0:T(8,128)(2,1)} %get-tuple-element.216, s32[]{:T(128)} %get-tuple-element.203), kind=kOutput, calls=%fused_computation.1.clone.1 | convolution fusion | flops 269481984 | bytes 4858368 | tf_op jit(solution)/shard_map/while/body/eval_jaxpr/rkgd,skd->krgs/dot_general | solution.py:68
  184.1 3.8 %fusion.44 = f32[1,256,8,128]{3,1,2,0:T(8,128)S(1)} fusion(f32[512,256,8]{1,0,2:T(8,128)} %get-tuple-element.192, f32[256,8]{0,1:T(8,128)S(1)} %bitcast.109, f32[1,256,8,128]{3,1,2,0:T(8,128)S(1)} %get-tuple-element.206, f32[256,8]{0,1:T(8,128)S(1)} %get-tuple-element.193, pred[]{:T(512)S(6)} %compare.3, ...), kind=kOutput, calls=%fused_computation.8.clone.1 | convolution fusion | flops 271319040 | bytes 6439425 | tf_op jit(solution)/shard_map/while/body/eval_jaxpr/krgs,skd->krgd/dot_general | solution.py:76
  187.9 0.6 fusion.43
  188.6 0.4 copy.72
  188.9 0.4 copy.73
  189.3 0.6 copy.89
  189.9 0.9 pad_maximum_fusion
  190.9 47.4 %all_to_all.39 = bf16[1,1,256,8,130]{4,3,1,0,2:T(8,128)(2,1)S(1)} all-to-all(bf16[1,1,256,8,130]{4,3,1,0,2:T(8,128)(2,1)S(1)} %pad_maximum_fusion), channel_id=1, replica_groups=mesh['groups'=2,'tok'=16,'head'=8,'row'=2] {'tok'}, dimensions={2} | all-to-all | bytes 1064960 | tf_op jit(solution)/shard_map/all_to_all | solution.py:37
  238.2 0.4 fusion.31
  238.7 0.8 copy.80
  239.6 0.8 copy.81
  240.6 0.1 copy.75
  240.7 0.5 multiply_reduce_fusion
  241.2 0.1 divide_convert_fusion
  241.4 29.5 %all_to_all.40 = bf16[16,16,1024]{2,1,0:T(8,128)(2,1)S(1)} all-to-all(bf16[16,16,1024]{2,1,0:T(8,128)(2,1)S(1)} %broadcast_in_dim.18), channel_id=1, replica_groups=mesh['groups'=2,'tok'=16,'head'=8,'row'=2] {'tok'}, dimensions={0} | all-to-all | bytes 1048576 | tf_op jit(solution)/shard_map/all_to_all | solution.py:12
  270.9 2.4 convolution_convert_fusion.1
  273.2 7.6 %all-to-all-start.4 = ((bf16[8,32,512]{2,1,0:T(8,128)(2,1)}), bf16[8,32,512]{2,1,0:T(8,128)(2,1)S(1)}, u32[]{:S(2)}, u32[]{:S(2)}) async-start(bf16[8,32,512]{2,1,0:T(8,128)(2,1)} %bitcast.13), calls=%async_computation.4 | async-start | bytes 524288 | tf_op jit(solution)/shard_map/all_to_all | solution.py:29
  281.6 10.8 %all-to-all-done.4 = bf16[8,32,512]{2,1,0:T(8,128)(2,1)S(1)} async-done(((bf16[8,32,512]{2,1,0:T(8,128)(2,1)}), bf16[8,32,512]{2,1,0:T(8,128)(2,1)S(1)}, u32[]{:S(2)}, u32[]{:S(2)}) %all-to-all-start.4) | async-done | bytes 262176 | tf_op jit(solution)/shard_map/all_to_all | solution.py:29
  292.5 13.3 %all_to_all.41 = bf16[8,32,512]{2,1,0:T(8,128)(2,1)S(1)} all-to-all(bf16[8,32,512]{2,1,0:T(8,128)(2,1)S(1)} %broadcast_in_dim.19), channel_id=1, replica_groups=mesh['groups'=2,'tok'=16,'head'=8,'row'=2] {'head'}, dimensions={0} | all-to-all | bytes 524288 | tf_op jit(solution)/shard_map/all_to_all | solution.py:12
  305.8 0.7 copy.105
  (66 shorter events, 0.9 us)
Async XLA Ops:
  0.0 57.0 %copy-start = (bf16[512,1024]{1,0:T(8,128)(2,1)S(1)}, bf16[512,1024]{1,0:T(8,128)(2,1)}, u32[]{:S(2)}) copy-start(bf16[512,1024]{1,0:T(8,128)(2,1)} %param.9) | copy-start | bytes 3145732
  59.3 30.8 %all-to-all-start.1 = ((bf16[16,16,1024]{2,1,0:T(8,128)(2,1)}), bf16[16,16,1024]{2,1,0:T(8,128)(2,1)S(1)}, u32[]{:S(2)}, u32[]{:S(2)}) async-start(bf16[16,16,1024]{2,1,0:T(8,128)(2,1)} %bitcast.2), calls=%async_computation.1 | async-start | bytes 1048576 | tf_op jit(solution)/shard_map/all_to_all | solution.py:29
  127.9 3.8 %copy-start.1 = (f32[512,256,8]{1,0,2:T(8,128)S(1)}, f32[512,256,8]{1,0,2:T(8,128)}, u32[]{:S(2)}) copy-start(f32[512,256,8]{1,0,2:T(8,128)} %get-tuple-element.192) | copy-start | bytes 12582916 | tf_op jit(solution)/shard_map/while
  136.0 3.8 %copy-start.1 = (f32[512,256,8]{1,0,2:T(8,128)S(1)}, f32[512,256,8]{1,0,2:T(8,128)}, u32[]{:S(2)}) copy-start(f32[512,256,8]{1,0,2:T(8,128)} %get-tuple-element.192) | copy-start | bytes 12582916 | tf_op jit(solution)/shard_map/while
  144.0 3.8 %copy-start.1 = (f32[512,256,8]{1,0,2:T(8,128)S(1)}, f32[512,256,8]{1,0,2:T(8,128)}, u32[]{:S(2)}) copy-start(f32[512,256,8]{1,0,2:T(8,128)} %get-tuple-element.192) | copy-start | bytes 12582916 | tf_op jit(solution)/shard_map/while
  152.0 3.8 %copy-start.1 = (f32[512,256,8]{1,0,2:T(8,128)S(1)}, f32[512,256,8]{1,0,2:T(8,128)}, u32[]{:S(2)}) copy-start(f32[512,256,8]{1,0,2:T(8,128)} %get-tuple-element.192) | copy-start | bytes 12582916 | tf_op jit(solution)/shard_map/while
  160.0 3.8 %copy-start.1 = (f32[512,256,8]{1,0,2:T(8,128)S(1)}, f32[512,256,8]{1,0,2:T(8,128)}, u32[]{:S(2)}) copy-start(f32[512,256,8]{1,0,2:T(8,128)} %get-tuple-element.192) | copy-start | bytes 12582916 | tf_op jit(solution)/shard_map/while
  168.0 3.8 %copy-start.1 = (f32[512,256,8]{1,0,2:T(8,128)S(1)}, f32[512,256,8]{1,0,2:T(8,128)}, u32[]{:S(2)}) copy-start(f32[512,256,8]{1,0,2:T(8,128)} %get-tuple-element.192) | copy-start | bytes 12582916 | tf_op jit(solution)/shard_map/while
  176.1 3.8 %copy-start.1 = (f32[512,256,8]{1,0,2:T(8,128)S(1)}, f32[512,256,8]{1,0,2:T(8,128)}, u32[]{:S(2)}) copy-start(f32[512,256,8]{1,0,2:T(8,128)} %get-tuple-element.192) | copy-start | bytes 12582916 | tf_op jit(solution)/shard_map/while
  184.1 3.8 %copy-start.1 = (f32[512,256,8]{1,0,2:T(8,128)S(1)}, f32[512,256,8]{1,0,2:T(8,128)}, u32[]{:S(2)}) copy-start(f32[512,256,8]{1,0,2:T(8,128)} %get-tuple-element.192) | copy-start | bytes 12582916 | tf_op jit(solution)/shard_map/while
  238.2 42.6 %copy-start.2 = (bf16[256,512]{1,0:T(8,128)(2,1)S(1)}, bf16[256,512]{1,0:T(8,128)(2,1)}, u32[]{:S(2)}) copy-start(bf16[256,512]{1,0:T(8,128)(2,1)} %param.8) | copy-start | bytes 786436
  273.2 19.2 %all-to-all-start.4 = ((bf16[8,32,512]{2,1,0:T(8,128)(2,1)}), bf16[8,32,512]{2,1,0:T(8,128)(2,1)S(1)}, u32[]{:S(2)}, u32[]{:S(2)}) async-start(bf16[8,32,512]{2,1,0:T(8,128)(2,1)} %bitcast.13), calls=%async_computation.4 | async-start | bytes 524288 | tf_op jit(solution)/shard_map/all_to_all | solution.py:29
where the time goes:
time: 307 us
  blocking collectives  180 us (59%)
  matrix products  63.6 us (21%)
  waiting for transfers between devices  37.6 us (12%)
  starting transfers between devices  11.7 us (4%)
  other arithmetic  8.17 us (3%)
  local copies, waits for them, and re-layouts  4.22 us (1%)
    all_to_all x3, blocking collectives, copy_for_each(): lax.all_to_all(jnp.broadcast_to(array[None], (devices, *array.shape)), ax...  98.6 us
    all_to_all x1, blocking collectives, side_by_side(): lax.all_to_all(both, axis, split_axis=split_dim, concat_axis=concat_dim,...  47.4 us
    all_to_all x2, waiting for transfers between devices, sum_at_owner(): lax.all_to_all(parts, axis, split_axis=0, concat_axis=0, tiled=True)  37.6 us
    all_gather x1, blocking collectives, body(): queries = lax.all_gather(share_queries, 'tok', axis=0, tiled=True)  34.1 us
    dot_general x8, matrix products, step(): jnp.einsum('krgs,skd->krgd', rounded, value_block, preferred_element_type...  30.6 us
    dot_general x8, matrix products, step(): jnp.einsum('rkgd,skd->krgs', queries, key_block, preferred_element_type=j...  28.4 us
    all_to_all x2, starting transfers between devices, sum_at_owner(): lax.all_to_all(parts, axis, split_axis=0, concat_axis=0, tiled=True)  11.7 us
  transfers between devices with their start and end apart: 2, of which 2 were waited for; matrix products, arithmetic and copies ran while one was open for 0% of the time, Pallas kernels for 0%

commit v1 on v0

--- a/solution.py
+++ b/solution.py
@@ -115,7 +115,9 @@
     rows = projected.shape[0]
     view = projected.reshape(rows, local_kv, GROUP, HD)
     share_queries = (view / jnp.sqrt(jnp.float32(HD))).astype(jnp.bfloat16)
-    queries = lax.all_gather(share_queries, "tok", axis=0, tiled=True)
+    queries = jnp.concatenate(
+        lax.all_to_all(jnp.stack([share_queries] * lax.axis_size("tok")), "tok", 0, 0), axis=0
+    )
     running, total, accum = attend(queries, keys, values, empty_state(normed.shape[0], local_kv))
     pieces = tuple(
         (

time: 307 us -> 323 us (1.052)
  blocking collectives: 180 us -> 191 us
    all_gather x1 -> x0, blocking collectives: 34.1 us -> none  [body(): queries = lax.all_gather(share_queries, 'tok', axis=0, tiled=True)]
    all_to_all x0 -> x1, blocking collectives: none -> 29.9 us  [sum_at_owner(): lax.all_to_all(parts, axis, split_axis=0, concat_axis=0, tiled=True)]
    all_to_all x0 -> x1, waiting for transfers between devices: none -> 28.7 us  [body(): lax.all_to_all(jnp.stack([share_queries] * lax.axis_size('tok')), 'tok',...]
    all_to_all x2 -> x1, waiting for transfers between devices: 37.6 us -> 9.93 us  [sum_at_owner(): lax.all_to_all(parts, axis, split_axis=0, concat_axis=0, tiled=True)]
    all_to_all x1, blocking collectives: 47.4 us -> 57.6 us  [side_by_side(): lax.all_to_all(both, axis, split_axis=split_dim, concat_axis=concat_dim,...]
    all_to_all x0 -> x1, starting transfers between devices: none -> 7.34 us  [body(): lax.all_to_all(jnp.stack([share_queries] * lax.axis_size('tok')), 'tok',...]
    all_to_all x3, blocking collectives: 98.6 us -> 104 us  [copy_for_each(): lax.all_to_all(jnp.broadcast_to(array[None], (devices, *array.shape)), ax...]
    all_to_all x2 -> x1, starting transfers between devices: 11.7 us -> 7.32 us  [sum_at_owner(): lax.all_to_all(parts, axis, split_axis=0, concat_axis=0, tiled=True)]
where the time goes in v1:
time: 323 us; the launch traced here: 322 us
  blocking collectives  191 us (59%)
  matrix products  62.8 us (19%)
  waiting for transfers between devices  38.6 us (12%)
  starting transfers between devices  14.7 us (5%)
  other arithmetic  8.17 us (3%)
  local copies, waits for them, and re-layouts  5.24 us (2%)
    all_to_all x3, blocking collectives, copy_for_each(): lax.all_to_all(jnp.broadcast_to(array[None], (devices, *array.shape)), ax...  104 us
    all_to_all x1, blocking collectives, side_by_side(): lax.all_to_all(both, axis, split_axis=split_dim, concat_axis=concat_dim,...  57.6 us
    dot_general x8, matrix products, step(): jnp.einsum('krgs,skd->krgd', rounded, value_block, preferred_element_type...  30.6 us
    all_to_all x1, blocking collectives, sum_at_owner(): lax.all_to_all(parts, axis, split_axis=0, concat_axis=0, tiled=True)  29.9 us
    all_to_all x1, waiting for transfers between devices, body(): lax.all_to_all(jnp.stack([share_queries] * lax.axis_size('tok')), 'tok',...  28.7 us
    dot_general x8, matrix products, step(): jnp.einsum('rkgd,skd->krgs', queries, key_block, preferred_element_type=j...  28.4 us
    all_to_all x1, waiting for transfers between devices, sum_at_owner(): lax.all_to_all(parts, axis, split_axis=0, concat_axis=0, tiled=True)  9.93 us
    all_to_all x1, starting transfers between devices, body(): lax.all_to_all(jnp.stack([share_queries] * lax.axis_size('tok')), 'tok',...  7.34 us
  transfers between devices with their start and end apart: 2, of which 2 were waited for; matrix products, arithmetic and copies ran while one was open for 0% of the time, Pallas kernels for 0%

profile of v1, /device:TPU:80, one launch (start us, length us, event | category | flops | bytes accessed | tf_op | source)
XLA Modules:
  0.0 322.0 jit_solution(6308752470278187514)
XLA Ops:
  0.0 1.2 multiply_reduce_fusion.1
  1.2 55.8 %all_to_all.43 = f32[16,1,256]{2,1,0:T(1,128)S(1)} all-to-all(f32[16,1,256]{2,1,0:T(1,128)S(1)} %broadcast_in_dim.17), channel_id=1, replica_groups=mesh['groups'=2,'tok'=16,'head'=8,'row'=2] {'tok'}, dimensions={0} | all-to-all | bytes 32768 | tf_op jit(solution)/shard_map/all_to_all | solution.py:12
  57.0 1.4 convolution_convert_fusion
  58.5 29.9 %all_to_all.44 = bf16[16,16,1024]{2,1,0:T(8,128)(2,1)S(1)} all-to-all(bf16[16,16,1024]{2,1,0:T(8,128)(2,1)S(1)} %bitcast.111), channel_id=1, replica_groups=mesh['groups'=2,'tok'=16,'head'=8,'row'=2] {'tok'}, dimensions={0} | all-to-all | bytes 1048576 | tf_op jit(solution)/shard_map/all_to_all | solution.py:29
  88.5 0.9 stack.2
  89.4 7.3 %all-to-all-start.2 = ((bf16[16,16,1,8,128]{4,1,3,2,0:T(8,128)(2,1)}), bf16[16,16,1,8,128]{4,1,3,2,0:T(8,128)(2,1)S(1)}, u32[]{:S(2)}, u32[]{:S(2)}) async-start(bf16[16,16,1,8,128]{4,1,3,2,0:T(8,128)(2,1)} %stack.2), calls=%async_computation.2 | async-start | bytes 1048576 | tf_op jit(solution)/shard_map/all_to_all | solution.py:119
  96.8 28.7 %all-to-all-done.2 = bf16[16,16,1,8,128]{4,1,3,2,0:T(8,128)(2,1)S(1)} async-done(((bf16[16,16,1,8,128]{4,1,3,2,0:T(8,128)(2,1)}), bf16[16,16,1,8,128]{4,1,3,2,0:T(8,128)(2,1)S(1)}, u32[]{:S(2)}, u32[]{:S(2)}) %all-to-all-start.2) | async-done | bytes 524320 | tf_op jit(solution)/shard_map/all_to_all | solution.py:119
  125.5 0.1 copy.84
  125.7 64.2 %while.15 = (s32[]{:T(128)}, f32[1,256,8]{1,2,0:T(8,128)S(1)}, f32[1,256,8]{1,2,0:T(8,128)S(1)}, f32[1,256,8,128]{3,1,2,0:T(8,128)S(1)}, bf16[8,512,1,128]{3,1,2...) while((s32[]{:T(128)}, f32[1,256,8]{1,2,0:T(8,128)S(1)}, ...), condition=%wide.region_6.7_spmd.clone, body=%wide.region_3.6_spmd.clone.sunk | while | flops 542912512 | bytes 32375940 | solution.py:81
  125.7 3.5 %bitcast_reduce_fusion.2 = (f32[256,8]{0,1:T(8,128)S(1)}, f32[512,256,8]{1,0,2:T(8,128)}) fusion(bf16[256,1,8,128]{3,0,2,1:T(8,128)(2,1)S(1)} %get-tuple-element.196, bf16[8,512,1,128]{3,1,2,0:T(8,128)(2,1)} %get-tuple-element.195, s32[]{:T(128)} %get-tuple-element.182), kind=kOutput, calls=%fused_computation.1.clone.1 | convolution fusion | flops 269481984 | bytes 4858368 | tf_op jit(solution)/shard_map/while/body/eval_jaxpr/rkgd,skd->krgs/dot_general | solution.py:68
  129.3 3.8 %fusion.45 = f32[1,256,8,128]{3,1,2,0:T(8,128)S(1)} fusion(f32[512,256,8]{1,0,2:T(8,128)} %get-tuple-element.171, f32[256,8]{0,1:T(8,128)S(1)} %bitcast.108, f32[1,256,8,128]{3,1,2,0:T(8,128)S(1)} %get-tuple-element.185, f32[256,8]{0,1:T(8,128)S(1)} %get-tuple-element.172, pred[]{:T(512)S(6)} %compare.3, ...), kind=kOutput, calls=%fused_computation.8.clone.1 | convolution fusion | flops 271319040 | bytes 6439425 | tf_op jit(solution)/shard_map/while/body/eval_jaxpr/krgs,skd->krgd/dot_general | solution.py:76
  133.1 0.6 fusion.44
  133.7 3.5 %bitcast_reduce_fusion.2 = (f32[256,8]{0,1:T(8,128)S(1)}, f32[512,256,8]{1,0,2:T(8,128)}) fusion(bf16[256,1,8,128]{3,0,2,1:T(8,128)(2,1)S(1)} %get-tuple-element.196, bf16[8,512,1,128]{3,1,2,0:T(8,128)(2,1)} %get-tuple-element.195, s32[]{:T(128)} %get-tuple-element.182), kind=kOutput, calls=%fused_computation.1.clone.1 | convolution fusion | flops 269481984 | bytes 4858368 | tf_op jit(solution)/shard_map/while/body/eval_jaxpr/rkgd,skd->krgs/dot_general | solution.py:68
  137.3 3.8 %fusion.45 = f32[1,256,8,128]{3,1,2,0:T(8,128)S(1)} fusion(f32[512,256,8]{1,0,2:T(8,128)} %get-tuple-element.171, f32[256,8]{0,1:T(8,128)S(1)} %bitcast.108, f32[1,256,8,128]{3,1,2,0:T(8,128)S(1)} %get-tuple-element.185, f32[256,8]{0,1:T(8,128)S(1)} %get-tuple-element.172, pred[]{:T(512)S(6)} %compare.3, ...), kind=kOutput, calls=%fused_computation.8.clone.1 | convolution fusion | flops 271319040 | bytes 6439425 | tf_op jit(solution)/shard_map/while/body/eval_jaxpr/krgs,skd->krgd/dot_general | solution.py:76
  141.1 0.6 fusion.44
  141.7 3.5 %bitcast_reduce_fusion.2 = (f32[256,8]{0,1:T(8,128)S(1)}, f32[512,256,8]{1,0,2:T(8,128)}) fusion(bf16[256,1,8,128]{3,0,2,1:T(8,128)(2,1)S(1)} %get-tuple-element.196, bf16[8,512,1,128]{3,1,2,0:T(8,128)(2,1)} %get-tuple-element.195, s32[]{:T(128)} %get-tuple-element.182), kind=kOutput, calls=%fused_computation.1.clone.1 | convolution fusion | flops 269481984 | bytes 4858368 | tf_op jit(solution)/shard_map/while/body/eval_jaxpr/rkgd,skd->krgs/dot_general | solution.py:68
  145.3 3.8 %fusion.45 = f32[1,256,8,128]{3,1,2,0:T(8,128)S(1)} fusion(f32[512,256,8]{1,0,2:T(8,128)} %get-tuple-element.171, f32[256,8]{0,1:T(8,128)S(1)} %bitcast.108, f32[1,256,8,128]{3,1,2,0:T(8,128)S(1)} %get-tuple-element.185, f32[256,8]{0,1:T(8,128)S(1)} %get-tuple-element.172, pred[]{:T(512)S(6)} %compare.3, ...), kind=kOutput, calls=%fused_computation.8.clone.1 | convolution fusion | flops 271319040 | bytes 6439425 | tf_op jit(solution)/shard_map/while/body/eval_jaxpr/krgs,skd->krgd/dot_general | solution.py:76
  149.1 0.6 fusion.44
  149.8 3.5 %bitcast_reduce_fusion.2 = (f32[256,8]{0,1:T(8,128)S(1)}, f32[512,256,8]{1,0,2:T(8,128)}) fusion(bf16[256,1,8,128]{3,0,2,1:T(8,128)(2,1)S(1)} %get-tuple-element.196, bf16[8,512,1,128]{3,1,2,0:T(8,128)(2,1)} %get-tuple-element.195, s32[]{:T(128)} %get-tuple-element.182), kind=kOutput, calls=%fused_computation.1.clone.1 | convolution fusion | flops 269481984 | bytes 4858368 | tf_op jit(solution)/shard_map/while/body/eval_jaxpr/rkgd,skd->krgs/dot_general | solution.py:68
  153.3 3.8 %fusion.45 = f32[1,256,8,128]{3,1,2,0:T(8,128)S(1)} fusion(f32[512,256,8]{1,0,2:T(8,128)} %get-tuple-element.171, f32[256,8]{0,1:T(8,128)S(1)} %bitcast.108, f32[1,256,8,128]{3,1,2,0:T(8,128)S(1)} %get-tuple-element.185, f32[256,8]{0,1:T(8,128)S(1)} %get-tuple-element.172, pred[]{:T(512)S(6)} %compare.3, ...), kind=kOutput, calls=%fused_computation.8.clone.1 | convolution fusion | flops 271319040 | bytes 6439425 | tf_op jit(solution)/shard_map/while/body/eval_jaxpr/krgs,skd->krgd/dot_general | solution.py:76
  157.1 0.6 fusion.44
  157.8 3.5 %bitcast_reduce_fusion.2 = (f32[256,8]{0,1:T(8,128)S(1)}, f32[512,256,8]{1,0,2:T(8,128)}) fusion(bf16[256,1,8,128]{3,0,2,1:T(8,128)(2,1)S(1)} %get-tuple-element.196, bf16[8,512,1,128]{3,1,2,0:T(8,128)(2,1)} %get-tuple-element.195, s32[]{:T(128)} %get-tuple-element.182), kind=kOutput, calls=%fused_computation.1.clone.1 | convolution fusion | flops 269481984 | bytes 4858368 | tf_op jit(solution)/shard_map/while/body/eval_jaxpr/rkgd,skd->krgs/dot_general | solution.py:68
  161.3 3.8 %fusion.45 = f32[1,256,8,128]{3,1,2,0:T(8,128)S(1)} fusion(f32[512,256,8]{1,0,2:T(8,128)} %get-tuple-element.171, f32[256,8]{0,1:T(8,128)S(1)} %bitcast.108, f32[1,256,8,128]{3,1,2,0:T(8,128)S(1)} %get-tuple-element.185, f32[256,8]{0,1:T(8,128)S(1)} %get-tuple-element.172, pred[]{:T(512)S(6)} %compare.3, ...), kind=kOutput, calls=%fused_computation.8.clone.1 | convolution fusion | flops 271319040 | bytes 6439425 | tf_op jit(solution)/shard_map/while/body/eval_jaxpr/krgs,skd->krgd/dot_general | solution.py:76
  165.2 0.6 fusion.44
  165.8 3.5 %bitcast_reduce_fusion.2 = (f32[256,8]{0,1:T(8,128)S(1)}, f32[512,256,8]{1,0,2:T(8,128)}) fusion(bf16[256,1,8,128]{3,0,2,1:T(8,128)(2,1)S(1)} %get-tuple-element.196, bf16[8,512,1,128]{3,1,2,0:T(8,128)(2,1)} %get-tuple-element.195, s32[]{:T(128)} %get-tuple-element.182), kind=kOutput, calls=%fused_computation.1.clone.1 | convolution fusion | flops 269481984 | bytes 4858368 | tf_op jit(solution)/shard_map/while/body/eval_jaxpr/rkgd,skd->krgs/dot_general | solution.py:68
  169.3 3.8 %fusion.45 = f32[1,256,8,128]{3,1,2,0:T(8,128)S(1)} fusion(f32[512,256,8]{1,0,2:T(8,128)} %get-tuple-element.171, f32[256,8]{0,1:T(8,128)S(1)} %bitcast.108, f32[1,256,8,128]{3,1,2,0:T(8,128)S(1)} %get-tuple-element.185, f32[256,8]{0,1:T(8,128)S(1)} %get-tuple-element.172, pred[]{:T(512)S(6)} %compare.3, ...), kind=kOutput, calls=%fused_computation.8.clone.1 | convolution fusion | flops 271319040 | bytes 6439425 | tf_op jit(solution)/shard_map/while/body/eval_jaxpr/krgs,skd->krgd/dot_general | solution.py:76
  173.2 0.6 fusion.44
  173.8 3.5 %bitcast_reduce_fusion.2 = (f32[256,8]{0,1:T(8,128)S(1)}, f32[512,256,8]{1,0,2:T(8,128)}) fusion(bf16[256,1,8,128]{3,0,2,1:T(8,128)(2,1)S(1)} %get-tuple-element.196, bf16[8,512,1,128]{3,1,2,0:T(8,128)(2,1)} %get-tuple-element.195, s32[]{:T(128)} %get-tuple-element.182), kind=kOutput, calls=%fused_computation.1.clone.1 | convolution fusion | flops 269481984 | bytes 4858368 | tf_op jit(solution)/shard_map/while/body/eval_jaxpr/rkgd,skd->krgs/dot_general | solution.py:68
  177.4 3.8 %fusion.45 = f32[1,256,8,128]{3,1,2,0:T(8,128)S(1)} fusion(f32[512,256,8]{1,0,2:T(8,128)} %get-tuple-element.171, f32[256,8]{0,1:T(8,128)S(1)} %bitcast.108, f32[1,256,8,128]{3,1,2,0:T(8,128)S(1)} %get-tuple-element.185, f32[256,8]{0,1:T(8,128)S(1)} %get-tuple-element.172, pred[]{:T(512)S(6)} %compare.3, ...), kind=kOutput, calls=%fused_computation.8.clone.1 | convolution fusion | flops 271319040 | bytes 6439425 | tf_op jit(solution)/shard_map/while/body/eval_jaxpr/krgs,skd->krgd/dot_general | solution.py:76
  181.2 0.6 fusion.44
  181.8 3.5 %bitcast_reduce_fusion.2 = (f32[256,8]{0,1:T(8,128)S(1)}, f32[512,256,8]{1,0,2:T(8,128)}) fusion(bf16[256,1,8,128]{3,0,2,1:T(8,128)(2,1)S(1)} %get-tuple-element.196, bf16[8,512,1,128]{3,1,2,0:T(8,128)(2,1)} %get-tuple-element.195, s32[]{:T(128)} %get-tuple-element.182), kind=kOutput, calls=%fused_computation.1.clone.1 | convolution fusion | flops 269481984 | bytes 4858368 | tf_op jit(solution)/shard_map/while/body/eval_jaxpr/rkgd,skd->krgs/dot_general | solution.py:68
  185.4 3.8 %fusion.45 = f32[1,256,8,128]{3,1,2,0:T(8,128)S(1)} fusion(f32[512,256,8]{1,0,2:T(8,128)} %get-tuple-element.171, f32[256,8]{0,1:T(8,128)S(1)} %bitcast.108, f32[1,256,8,128]{3,1,2,0:T(8,128)S(1)} %get-tuple-element.185, f32[256,8]{0,1:T(8,128)S(1)} %get-tuple-element.172, pred[]{:T(512)S(6)} %compare.3, ...), kind=kOutput, calls=%fused_computation.8.clone.1 | convolution fusion | flops 271319040 | bytes 6439425 | tf_op jit(solution)/shard_map/while/body/eval_jaxpr/krgs,skd->krgd/dot_general | solution.py:76
  189.2 0.6 fusion.44
  189.9 0.4 copy.87
  190.2 0.4 copy.88
  190.6 0.6 copy.105
  191.2 0.9 pad_maximum_fusion
  192.1 57.6 %all_to_all.45 = bf16[1,1,256,8,130]{4,3,1,0,2:T(8,128)(2,1)S(1)} all-to-all(bf16[1,1,256,8,130]{4,3,1,0,2:T(8,128)(2,1)S(1)} %pad_maximum_fusion), channel_id=1, replica_groups=mesh['groups'=2,'tok'=16,'head'=8,'row'=2] {'tok'}, dimensions={2} | all-to-all | bytes 1064960 | tf_op jit(solution)/shard_map/all_to_all | solution.py:37
  249.7 0.4 fusion.31
  250.2 0.8 copy.95
  251.1 0.8 copy.96
  252.2 0.5 multiply_reduce_fusion
  252.8 35.0 %all_to_all.46 = bf16[16,16,1024]{2,1,0:T(8,128)(2,1)S(1)} all-to-all(bf16[16,16,1024]{2,1,0:T(8,128)(2,1)S(1)} %broadcast_in_dim.18), channel_id=1, replica_groups=mesh['groups'=2,'tok'=16,'head'=8,'row'=2] {'tok'}, dimensions={0} | all-to-all | bytes 1048576 | tf_op jit(solution)/shard_map/all_to_all | solution.py:12
  287.9 2.4 convolution_convert_fusion.1
  290.2 7.3 %all-to-all-start.5 = ((bf16[8,32,512]{2,1,0:T(8,128)(2,1)}), bf16[8,32,512]{2,1,0:T(8,128)(2,1)S(1)}, u32[]{:S(2)}, u32[]{:S(2)}) async-start(bf16[8,32,512]{2,1,0:T(8,128)(2,1)} %bitcast.13), calls=%async_computation.5 | async-start | bytes 524288 | tf_op jit(solution)/shard_map/all_to_all | solution.py:29
  298.3 9.9 %all-to-all-done.5 = bf16[8,32,512]{2,1,0:T(8,128)(2,1)S(1)} async-done(((bf16[8,32,512]{2,1,0:T(8,128)(2,1)}), bf16[8,32,512]{2,1,0:T(8,128)(2,1)S(1)}, u32[]{:S(2)}, u32[]{:S(2)}) %all-to-all-start.5) | async-done | bytes 262176 | tf_op jit(solution)/shard_map/all_to_all | solution.py:29
  308.3 12.9 %all_to_all.47 = bf16[8,32,512]{2,1,0:T(8,128)(2,1)S(1)} all-to-all(bf16[8,32,512]{2,1,0:T(8,128)(2,1)S(1)} %broadcast_in_dim.19), channel_id=1, replica_groups=mesh['groups'=2,'tok'=16,'head'=8,'row'=2] {'head'}, dimensions={0} | all-to-all | bytes 524288 | tf_op jit(solution)/shard_map/all_to_all | solution.py:12
  321.3 0.7 copy.121
  (67 shorter events, 1.0 us)
Async XLA Ops:
  0.0 57.0 %copy-start = (bf16[512,1024]{1,0:T(8,128)(2,1)S(1)}, bf16[512,1024]{1,0:T(8,128)(2,1)}, u32[]{:S(2)}) copy-start(bf16[512,1024]{1,0:T(8,128)(2,1)} %param.9) | copy-start | bytes 3145732
  89.4 36.1 %all-to-all-start.2 = ((bf16[16,16,1,8,128]{4,1,3,2,0:T(8,128)(2,1)}), bf16[16,16,1,8,128]{4,1,3,2,0:T(8,128)(2,1)S(1)}, u32[]{:S(2)}, u32[]{:S(2)}) async-start(bf16[16,16,1,8,128]{4,1,3,2,0:T(8,128)(2,1)} %stack.2), calls=%async_computation.2 | async-start | bytes 1048576 | tf_op jit(solution)/shard_map/all_to_all | solution.py:119
  129.2 3.8 %copy-start.1 = (f32[512,256,8]{1,0,2:T(8,128)S(1)}, f32[512,256,8]{1,0,2:T(8,128)}, u32[]{:S(2)}) copy-start(f32[512,256,8]{1,0,2:T(8,128)} %get-tuple-element.171) | copy-start | bytes 12582916 | tf_op jit(solution)/shard_map/while
  137.3 3.8 %copy-start.1 = (f32[512,256,8]{1,0,2:T(8,128)S(1)}, f32[512,256,8]{1,0,2:T(8,128)}, u32[]{:S(2)}) copy-start(f32[512,256,8]{1,0,2:T(8,128)} %get-tuple-element.171) | copy-start | bytes 12582916 | tf_op jit(solution)/shard_map/while
  145.3 3.8 %copy-start.1 = (f32[512,256,8]{1,0,2:T(8,128)S(1)}, f32[512,256,8]{1,0,2:T(8,128)}, u32[]{:S(2)}) copy-start(f32[512,256,8]{1,0,2:T(8,128)} %get-tuple-element.171) | copy-start | bytes 12582916 | tf_op jit(solution)/shard_map/while
  153.3 3.8 %copy-start.1 = (f32[512,256,8]{1,0,2:T(8,128)S(1)}, f32[512,256,8]{1,0,2:T(8,128)}, u32[]{:S(2)}) copy-start(f32[512,256,8]{1,0,2:T(8,128)} %get-tuple-element.171) | copy-start | bytes 12582916 | tf_op jit(solution)/shard_map/while
  161.3 3.8 %copy-start.1 = (f32[512,256,8]{1,0,2:T(8,128)S(1)}, f32[512,256,8]{1,0,2:T(8,128)}, u32[]{:S(2)}) copy-start(f32[512,256,8]{1,0,2:T(8,128)} %get-tuple-element.171) | copy-start | bytes 12582916 | tf_op jit(solution)/shard_map/while
  169.3 3.8 %copy-start.1 = (f32[512,256,8]{1,0,2:T(8,128)S(1)}, f32[512,256,8]{1,0,2:T(8,128)}, u32[]{:S(2)}) copy-start(f32[512,256,8]{1,0,2:T(8,128)} %get-tuple-element.171) | copy-start | bytes 12582916 | tf_op jit(solution)/shard_map/while
  177.4 3.8 %copy-start.1 = (f32[512,256,8]{1,0,2:T(8,128)S(1)}, f32[512,256,8]{1,0,2:T(8,128)}, u32[]{:S(2)}) copy-start(f32[512,256,8]{1,0,2:T(8,128)} %get-tuple-element.171) | copy-start | bytes 12582916 | tf_op jit(solution)/shard_map/while
  185.4 3.8 %copy-start.1 = (f32[512,256,8]{1,0,2:T(8,128)S(1)}, f32[512,256,8]{1,0,2:T(8,128)}, u32[]{:S(2)}) copy-start(f32[512,256,8]{1,0,2:T(8,128)} %get-tuple-element.171) | copy-start | bytes 12582916 | tf_op jit(solution)/shard_map/while
  249.7 47.9 %copy-start.2 = (bf16[256,512]{1,0:T(8,128)(2,1)S(1)}, bf16[256,512]{1,0:T(8,128)(2,1)}, u32[]{:S(2)}) copy-start(bf16[256,512]{1,0:T(8,128)(2,1)} %param.8) | copy-start | bytes 786436
  290.2 18.0 %all-to-all-start.5 = ((bf16[8,32,512]{2,1,0:T(8,128)(2,1)}), bf16[8,32,512]{2,1,0:T(8,128)(2,1)S(1)}, u32[]{:S(2)}, u32[]{:S(2)}) async-start(bf16[8,32,512]{2,1,0:T(8,128)(2,1)} %bitcast.13), calls=%async_computation.5 | async-start | bytes 524288 | tf_op jit(solution)/shard_map/all_to_all | solution.py:29
